TPU v7x, 512 devices: a whole 4x4x16 slice. The times are simulated.
512 devices in a mesh: row: 16 (over z), col: 16 (over y, x), layer: 2 (over core).
Axes of the slice: x: 4, y: 4, z: 16, core: 2. Of those that a mesh axis runs over, the one named last changes fastest.
Arguments:
- ratings: bfloat16 [32768, 16384], P('row', ('col', 'layer')), may hold values from -6 to 6
- tile_mask: int32 [256, 128], P('row', ('col', 'layer')), may hold values 0 or 1
- tile_counts: int32 [256, 128], P('row', ('col', 'layer')), may hold values from 1 to 16384
- user_factor: float32 [256, 32768], P(('col', 'layer'), 'row'), may hold values from -1.5 to 1.5
- item_factor: float32 [256, 16384], P('row', ('col', 'layer')), may hold values from -1.5 to 1.5
Outputs:
- new_user: float32 [256, 32768], P(('col', 'layer'), 'row')
- new_item: float32 [256, 16384], P('row', ('col', 'layer'))
- loss_value: float32 [], replicated
- grad_norm: float32 [], replicated
All inputs are finite; a program needn't handle non-finite values. No bound on the sum of `tile_mask` on one device may be relied on, other than what follows from the above.
Results may differ from a plain program's by a relative error of at most 0.0049.
Values may be sent and summed in bfloat16 or wider, within the bound.
No kernel may reach another device: no remote copies, remote signals or barrier semaphores. Data moves between devices by JAX's collectives and lax.ppermute only.
A program may use at most 64 MiB of HBM per device.

v0:
```python
import jax
import jax.numpy as jnp
from jax import lax
from jax.experimental import pallas as pl
from jax.experimental.pallas import tpu as pltpu
from jax.sharding import Mesh
from jax.sharding import PartitionSpec as P

TILE = 128
LANES = 128
STRIPE = 512
GATHER_FIRST, SCATTER_FIRST = 0, 9
COL_LAYER = ("col_0", "col_1", "layer")
VMEM = pl.BlockSpec(memory_space=pltpu.VMEM)
SMEM = pl.BlockSpec(memory_space=pltpu.SMEM)
FAR = pl.BlockSpec(memory_space=pltpu.HBM)
GRANT = pltpu.CompilerParams(vmem_limit_bytes=16 * 2**20)
MOST_GRANT = pltpu.CompilerParams(vmem_limit_bytes=52 * 2**20)
WHOLE_GRANT = pltpu.CompilerParams(vmem_limit_bytes=60 * 2**20)

epsilon = 1e-12
trust_ratio = 0.2


def lower_body(user_ref, blocks_ref):
    user = user_ref[...].astype(jnp.bfloat16)
    blocks_ref[...] = jnp.broadcast_to(user[None], blocks_ref.shape)


def lowered_for_all(factor, devices):
    return pl.pallas_call(
        lower_body,
        in_specs=[VMEM],
        out_specs=VMEM,
        out_shape=jax.ShapeDtypeStruct((devices, *factor.shape), jnp.bfloat16),
        compiler_params=WHOLE_GRANT,
        name="lower",
    )(factor)


def residual_body(
    far_mask_ref, far_counts_ref, far_user_ref, far_item_ref, far_ratings_ref,
    scaled_ref, item_share_ref, error_ref,
    mask_ref, counts_ref, user_ref, item_ref, ratings_ref, total_ref, sems, ratings_sems,
):
    columns = ratings_ref.shape[1]
    starts = range(0, ratings_ref.shape[0], STRIPE)
    stripes = [pl.ds(start, STRIPE) for start in starts]
    rank = item_ref.shape[0]
    turn = GATHER_FIRST * rank // 16
    pairs = [(far_user_ref, user_ref), (far_mask_ref, mask_ref), (far_counts_ref, counts_ref)]
    pairs.append((far_item_ref.at[pl.ds(0, rank - turn)], item_ref.at[pl.ds(turn, rank - turn)]))
    if turn:
        pairs.append((far_item_ref.at[pl.ds(rank - turn, turn)], item_ref.at[pl.ds(0, turn)]))
    copies = [pltpu.make_async_copy(far, near, sems.at[at]) for at, (far, near) in enumerate(pairs)]
    ratings_copies = [
        pltpu.make_async_copy(far_ratings_ref.at[stripe], ratings_ref.at[stripe], ratings_sems.at[at])
        for at, stripe in enumerate(stripes)
    ]
    for copy in copies + ratings_copies:
        copy.start()
    for copy in copies:
        copy.wait()
    item = item_ref[...]
    side = (TILE, TILE)
    position = lax.broadcasted_iota(jnp.int32, side, 0) * TILE + lax.broadcasted_iota(jnp.int32, side, 1)

    def predicted_of(at):
        user = user_ref[:, stripes[at]]
        return lax.dot_general(user, item, (((0,), (0,)), ((), ())), preferred_element_type=jnp.float32)

    def add_share(at):
        share = jnp.dot(user_ref[:, stripes[at]], scaled_ref[stripes[at]], preferred_element_type=jnp.float32)
        if at > 0:
            share = share + total_ref[...]
        if at + 1 < len(stripes):
            total_ref[...] = share
        else:
            blocks = share.astype(jnp.bfloat16).reshape(item_share_ref.shape)
            first = SCATTER_FIRST * blocks.shape[0] // 16
            item_share_ref[...] = jnp.concatenate([blocks[first:], blocks[:first]]) if first else blocks

    predicted = predicted_of(0)
    errors = [jnp.zeros((8, TILE), jnp.float32)] * (columns // TILE)
    for at, start in enumerate(starts):
        ratings_copies[at].wait()
        following = predicted_of(at + 1) if at + 1 < len(stripes) else None
        for row in range(0, STRIPE, TILE):
            for column in range(0, columns, TILE):
                tile_at = (column // TILE, (start + row) // TILE)
                limit = jnp.where(mask_ref[tile_at] == 1, counts_ref[tile_at], 0)
                rows, cols = pl.ds(start + row, TILE), pl.ds(column, TILE)
                rating = ratings_ref[rows, cols].astype(jnp.float32)
                difference = predicted[row : row + TILE, column : column + TILE] - rating
                residual = jnp.where(position < limit, difference, 0.0)
                scaled_ref[rows, cols] = residual.astype(jnp.bfloat16)
                error = (residual * residual).reshape(TILE // 8, 8, TILE).sum(axis=0)
                errors[column // TILE] = errors[column // TILE] + error
        if at > 0:
            add_share(at - 1)
        predicted = following
    add_share(len(stripes) - 1)
    error_ref[...] = jnp.concatenate(errors, axis=1)


def residual_of(mask, counts, user, item, ratings, devices):
    rank, columns = item.shape
    flops = 4 * rank * ratings.size
    return pl.pallas_call(
        residual_body,
        in_specs=[FAR] * 5,
        out_specs=[VMEM] * 3,
        out_shape=[
            jax.ShapeDtypeStruct(ratings.shape, jnp.bfloat16),
            jax.ShapeDtypeStruct((devices, rank // devices, columns), jnp.bfloat16),
            jax.ShapeDtypeStruct((8, columns), jnp.float32),
        ],
        scratch_shapes=[
            pltpu.SMEM(mask.shape, jnp.int32),
            pltpu.SMEM(counts.shape, jnp.int32),
            pltpu.VMEM(user.shape, jnp.bfloat16),
            pltpu.VMEM(item.shape, jnp.bfloat16),
            pltpu.VMEM(ratings.shape, jnp.bfloat16),
            pltpu.VMEM((rank, columns), jnp.float32),
            pltpu.SemaphoreType.DMA((5,)),
            pltpu.SemaphoreType.DMA((ratings.shape[0] // STRIPE,)),
        ],
        cost_estimate=pl.CostEstimate(flops=flops, bytes_accessed=4 * ratings.size, transcendentals=0),
        compiler_params=MOST_GRANT,
        name="residual",
    )(mask, counts, user, item, ratings)


def user_share_body(layer_ref, item_ref, scaled_ref, mine_ref, other_ref):
    chips, height, _ = mine_ref.shape
    item = item_ref[...]
    first = layer_ref[0] == 0
    for start in range(0, scaled_ref.shape[0], STRIPE):
        stripe = pl.ds(start, STRIPE)
        share = lax.dot_general(item, scaled_ref[stripe], (((1,), (1,)), ((), ())), preferred_element_type=jnp.float32)
        share = share.reshape(chips, 2, height, STRIPE)
        for at in range(chips):
            even, odd = share[at, 0], share[at, 1]
            chip = (at + GATHER_FIRST * chips // 16) % chips
            mine_ref[chip, :, stripe] = jnp.where(first, even, odd).astype(jnp.bfloat16)
            other_ref[chip, :, stripe] = jnp.where(first, odd, even).astype(jnp.bfloat16)


def user_share_of(layer, item, scaled, height):
    shape = jax.ShapeDtypeStruct((item.shape[0] // height // 2, height, scaled.shape[0]), jnp.bfloat16)
    return pl.pallas_call(
        user_share_body,
        in_specs=[SMEM, VMEM, VMEM],
        out_specs=[VMEM, VMEM],
        out_shape=[shape, shape],
        cost_estimate=pl.CostEstimate(flops=2 * item.shape[0] * scaled.size, bytes_accessed=0, transcendentals=0),
        compiler_params=GRANT,
        name="user_share",
    )(layer, item, scaled)


def halves_body(mine_ref, arrived_ref, total_ref):
    total_ref[...] = (mine_ref[...].astype(jnp.float32) + arrived_ref[...].astype(jnp.float32)).astype(jnp.bfloat16)


def halves_summed(mine, arrived):
    return pl.pallas_call(
        halves_body,
        in_specs=[VMEM, VMEM],
        out_specs=VMEM,
        out_shape=jax.ShapeDtypeStruct(mine.shape, jnp.bfloat16),
        compiler_params=GRANT,
        name="halves",
    )(mine, arrived)


def summed(blocks_ref):
    total = blocks_ref[0].astype(jnp.float32)
    for i in range(1, blocks_ref.shape[0]):
        total = total + blocks_ref[i].astype(jnp.float32)
    return total


def item_raw_body(mask_ref, counts_ref, arrived_ref, user_ref, item_ref, error_ref, raw_ref, sums_ref):
    raw = summed(arrived_ref)
    raw_ref[...] = raw
    user, item = user_ref[...], item_ref[...]
    lane = lax.broadcasted_iota(jnp.int32, sums_ref.shape, 1)
    sums = jnp.zeros(sums_ref.shape, jnp.float32)
    for at, value in enumerate(
        (
            jnp.sum((mask_ref[...] * counts_ref[...]).astype(jnp.float32)),
            jnp.sum(user * user) + jnp.sum(item * item),
            jnp.sum(error_ref[...]),
            jnp.sum(raw * raw),
        )
    ):
        sums = jnp.where(lane == at, value, sums)
    sums_ref[...] = sums


def item_raw_of(mask, counts, arrived, user_factor, item_factor, error):
    return pl.pallas_call(
        item_raw_body,
        in_specs=[VMEM] * 6,
        out_specs=[VMEM, VMEM],
        out_shape=[
            jax.ShapeDtypeStruct(arrived.shape[1:], jnp.float32),
            jax.ShapeDtypeStruct((1, LANES), jnp.float32),
        ],
        compiler_params=GRANT,
        name="item_raw",
    )(mask, counts, arrived, user_factor, item_factor, error)


def user_raw_body(arrived_ref, sums_ref, raw_ref, packed_ref):
    raw = summed(arrived_ref)
    raw_ref[...] = raw
    lane = lax.broadcasted_iota(jnp.int32, sums_ref.shape, 1)
    sums = sums_ref[...] + jnp.where(lane == 3, jnp.sum(raw * raw), 0.0)
    packed_ref[...] = jnp.broadcast_to(sums[None], packed_ref.shape)


def user_raw_of(arrived, sums, devices):
    return pl.pallas_call(
        user_raw_body,
        in_specs=[VMEM, VMEM],
        out_specs=[VMEM, VMEM],
        out_shape=[
            jax.ShapeDtypeStruct(arrived.shape[1:], jnp.float32),
            jax.ShapeDtypeStruct((devices, *sums.shape), jnp.float32),
        ],
        compiler_params=GRANT,
        name="user_raw",
    )(arrived, sums)


def packed_again_body(arrived_ref, packed_ref):
    packed_ref[...] = jnp.broadcast_to(summed(arrived_ref)[None], packed_ref.shape)


def packed_again(arrived, devices):
    return pl.pallas_call(
        packed_again_body,
        in_specs=[VMEM],
        out_specs=VMEM,
        out_shape=jax.ShapeDtypeStruct((devices, *arrived.shape[1:]), jnp.float32),
        compiler_params=GRANT,
        name="packed_again",
    )(arrived)


def step_body(arrived_ref, user_ref, item_ref, raw_user_ref, raw_item_ref, new_user_ref, new_item_ref, loss_ref, norm_ref):
    sums = summed(arrived_ref)
    lane = lax.broadcasted_iota(jnp.int32, sums.shape, 1)

    def lane_at(at):
        return jnp.sum(jnp.where(lane == at, sums, 0.0), axis=1, keepdims=True)

    observed_total = jnp.maximum(lane_at(0), 1.0)
    scale = 2.0 / observed_total
    grad_norm = scale * jnp.sqrt(lane_at(3) + epsilon)
    step_size = trust_ratio * jnp.sqrt(lane_at(1) + epsilon) / grad_norm * scale
    new_user_ref[...] = user_ref[...] - step_size * raw_user_ref[...]
    new_item_ref[...] = item_ref[...] - step_size * raw_item_ref[...]
    loss_ref[0, 0] = jnp.sum(lane_at(2) / observed_total)
    norm_ref[0, 0] = jnp.sum(grad_norm)


def stepped(arrived, user_factor, item_factor, raw_user, raw_item):
    return pl.pallas_call(
        step_body,
        in_specs=[VMEM] * 5,
        out_specs=[VMEM, VMEM, SMEM, SMEM],
        out_shape=[
            jax.ShapeDtypeStruct(user_factor.shape, jnp.float32),
            jax.ShapeDtypeStruct(item_factor.shape, jnp.float32),
            jax.ShapeDtypeStruct((1, 1), jnp.float32),
            jax.ShapeDtypeStruct((1, 1), jnp.float32),
        ],
        compiler_params=GRANT,
        name="step",
    )(arrived, user_factor, item_factor, raw_user, raw_item)


def exchanged(blocks, axis, groups=None):
    return lax.all_to_all(blocks, axis, 0, 0, tiled=True, axis_index_groups=groups)


def listed_from(first, count):
    return [[(first + i) % count for i in range(count)]]


def shifted(array, axis, by):
    count = lax.axis_size(axis)
    return lax.ppermute(array, axis, [(i, (i + by) % count) for i in range(count)])


def body(ratings, tile_mask, tile_counts, user_factor, item_factor):
    rows, height = lax.axis_size("row"), user_factor.shape[0]
    gather_list, scatter_list = (listed_from(first * rows // 16, rows) for first in (GATHER_FIRST, SCATTER_FIRST))
    layer = lax.axis_index("layer").astype(jnp.int32)[None]
    mask, counts = tile_mask.T, tile_counts.T
    user = exchanged(lowered_for_all(user_factor, lax.axis_size(COL_LAYER)), COL_LAYER)
    user = user.reshape(-1, user_factor.shape[1])
    item = lax.all_gather(item_factor.astype(jnp.bfloat16), "row", axis=0, tiled=True, axis_index_groups=gather_list)
    scaled, item_share, error = residual_of(mask, counts, user, item, ratings, rows)
    item_arrived = exchanged(item_share, "row", scatter_list)
    my_share, other_share = user_share_of(layer, item, scaled, height)
    partner_share = shifted(other_share, "layer", 1)
    halves = halves_summed(my_share, partner_share)
    user_arrived = exchanged(halves, ("col_0", "col_1"))
    raw_item, sums = item_raw_of(mask, counts, item_arrived, user_factor, item_factor, error)
    raw_user, packed = user_raw_of(user_arrived, sums, lax.axis_size(COL_LAYER))
    packed = exchanged(packed, COL_LAYER)
    packed = packed_again(packed, rows)
    packed = exchanged(packed, "row", scatter_list)
    new_user, new_item, loss_value, grad_norm = stepped(packed, user_factor, item_factor, raw_user, raw_item)
    return (new_user, new_item, loss_value.reshape(()), grad_norm.reshape(()))


def solution(mesh):
    finer = Mesh(
        mesh.devices.reshape(mesh.shape["row"], 4, 4, mesh.shape["layer"]),
        ("row", "col_0", "col_1", "layer"),
    )
    return jax.shard_map(
        body,
        mesh=finer,
        in_specs=(
            P("row", COL_LAYER),
            P("row", COL_LAYER),
            P("row", COL_LAYER),
            P(COL_LAYER, "row"),
            P("row", COL_LAYER),
        ),
        out_specs=(P(COL_LAYER, "row"), P("row", COL_LAYER), P(), P()),
        check_vma=False,
    )
```

profile of v0, /device:TPU:1, one launch (start us, length us, event | category | flops | bytes accessed | tf_op | source)
XLA Modules:
  0.0 115.0 jit_solution(8464685468030675674)
XLA Ops:
  0.6 0.0 copy-start.2
  0.6 0.0 copy-start.4
  0.7 0.0 copy-start.3
  0.7 2.0 %lower.1 = bf16[32,8,2048]{2,1,0:T(8,128)(2,1)} custom-call(f32[8,2048]{1,0:T(8,128)} %user_ref.5), custom_call_target="tpu_custom_call" | custom-call | tf_op jit(solution)/shard_map/lower/pallas_call | solution.py:31
  2.6 10.4 %all-to-all-start = ((bf16[32,8,2048]{2,1,0:T(8,128)(2,1)}), bf16[32,8,2048]{2,1,0:T(8,128)(2,1)S(1)}, u32[]{:S(2)}, u32[]{:S(2)}) async-start(bf16[32,8,2048]{2,1,0:T(8,128)(2,1)} %lower.1), calls=%async_computation | async-start | bytes 2097152 | tf_op jit(solution)/shard_map/all_to_all | solution.py:287
  13.0 0.0 copy-done.2
  13.1 28.6 %all_gather.3.far_item_ref.item_ref = bf16[256,512]{1,0:T(8,128)(2,1)S(1)} all-gather(bf16[16,512]{1,0:T(8,128)(2,1)S(1)} %convert_element_type.3), channel_id=1, replica_groups={{0,32,64,96,128,160,192,224,256,288,320,352,384,416,448,480},{1,33,65,9..., dimensions={0}, use_global_device_ids=true | all-gather | bytes 278528 | tf_op jit(solution)/shard_map/all_gather | solution.py:306
  41.7 0.0 all-to-all-done
  41.7 0.0 copy-done.4
  41.7 0.0 copy-done.3
  41.7 4.8 %residual.1 = (bf16[2048,512]{1,0:T(8,128)(2,1)}, bf16[16,16,512]{2,1,0:T(8,128)(2,1)}, f32[8,512]{1,0:T(8,128)S(1)}) custom-call(s32[4,16]{1,0:T(4,128)S(1)} %bitcast.7, s32[4,16]{1,0:T(4,128)S(1)} %bitcast.9, bf16[256,2048]{1,0:T(8,128)(2,1)S(1)} %bitcast.6, bf16[256,512]{1,0:T(8,128)(2,1)S(1)} %all_gather.3.far_item_ref.item_ref, ...), custom_call_target="tpu_custom_call" | custom-call | flops 1073741824 | bytes 4194304 | tf_op jit(solution)/shard_map/residual/pallas_call | solution.py:109
  46.5 10.6 %all-to-all-start.2 = ((bf16[16,16,512]{2,1,0:T(8,128)(2,1)}), bf16[16,16,512]{2,1,0:T(8,128)(2,1)S(1)}, u32[]{:S(2)}, u32[]{:S(2)}) async-start(bf16[16,16,512]{2,1,0:T(8,128)(2,1)} %get-tuple-element.20), calls=%async_computation.2 | async-start | bytes 524288 | tf_op jit(solution)/shard_map/all_to_all | solution.py:287
  57.1 0.0 copy-start
  57.1 1.6 %copy-done = bf16[2048,512]{1,0:T(8,128)(2,1)S(1)} copy-done((bf16[2048,512]{1,0:T(8,128)(2,1)S(1)}, bf16[2048,512]{1,0:T(8,128)(2,1)}, u32[]{:S(2)}) %copy-start) | copy-done | bytes 2097176
  58.7 0.0 copy-start.1
  58.7 0.7 user_share.1
  59.4 9.1 %collective-permute-start = (bf16[16,8,2048]{2,1,0:T(8,128)(2,1)S(1)}, bf16[16,8,2048]{2,1,0:T(8,128)(2,1)S(1)}, u32[]{:S(2)}, u32[]{:S(2)}) collective-permute-start(bf16[16,8,2048]{2,1,0:T(8,128)(2,1)S(1)} %get-tuple-element.19), channel_id=1, source_target_pairs={{0,1},{1,0},{2,3},{3,2},{4,5},{5,4},{6,7},{7,6},{8,9},{9,8},{10,11... | collective-permute-start | bytes 1572872 | tf_op jit(solution)/shard_map/ppermute | solution.py:296
  68.5 1.5 %collective-permute-done.arrived_ref = bf16[16,8,2048]{2,1,0:T(8,128)(2,1)S(1)} collective-permute-done((bf16[16,8,2048]{2,1,0:T(8,128)(2,1)S(1)}, bf16[16,8,2048]{2,1,0:T(8,128)(2,1)S(1)}, u32[]{:S(2)}, u32[]{:S(2)}) %collective-permute-start) | collective-permute-done | bytes 524320 | tf_op jit(solution)/shard_map/ppermute | solution.py:296
  70.0 0.9 halves.1
  70.9 0.0 all-to-all-done.2.arrived_ref
  70.9 6.8 %all-to-all-start.1 = ((bf16[16,8,2048]{2,1,0:T(8,128)(2,1)}), bf16[16,8,2048]{2,1,0:T(8,128)(2,1)S(1)}, u32[]{:S(2)}, u32[]{:S(2)}) async-start(bf16[16,8,2048]{2,1,0:T(8,128)(2,1)} %halves.1), calls=%async_computation.1 | async-start | bytes 1048576 | tf_op jit(solution)/shard_map/all_to_all | solution.py:287
  77.7 0.0 copy-done.1
  77.8 0.2 item_raw.1
  77.9 9.1 %all-to-all-done.1.arrived_ref = bf16[16,8,2048]{2,1,0:T(8,128)(2,1)S(1)} async-done(((bf16[16,8,2048]{2,1,0:T(8,128)(2,1)}), bf16[16,8,2048]{2,1,0:T(8,128)(2,1)S(1)}, u32[]{:S(2)}, u32[]{:S(2)}) %all-to-all-start.1) | async-done | bytes 524320 | tf_op jit(solution)/shard_map/all_to_all | solution.py:287
  87.1 0.2 user_raw.1
  87.3 13.2 %all_to_all.25.arrived_ref = f32[32,1,128]{2,1,0:T(1,128)S(1)} all-to-all(f32[32,1,128]{2,1,0:T(1,128)S(1)} %get-tuple-element.23), channel_id=1, replica_groups=mesh['row'=16,'col_0'=4,'col_1'=4,'layer'=2] {'col_0','col_1','layer'}, dimensions={0} | all-to-all | bytes 32768 | tf_op jit(solution)/shard_map/all_to_all | solution.py:287
  100.5 13.7 %all_to_all.26.arrived_ref = f32[16,1,128]{2,1,0:T(1,128)S(1)} all-to-all(f32[16,1,128]{2,1,0:T(1,128)S(1)} %packed_again.1), channel_id=1, replica_groups={{288,320,352,384,416,448,480,0,32,64,96,128,160,192,224,256},{289,321,3..., dimensions={0} | all-to-all | bytes 16384 | tf_op jit(solution)/shard_map/all_to_all | solution.py:287
  114.2 0.8 step.1
  (2 shorter events, 0.0 us)
Async XLA Ops:
  0.6 12.4 %copy-start.2 = (f32[16,512]{1,0:T(8,128)S(1)}, f32[16,512]{1,0:T(8,128)}, u32[]{:S(2)}) copy-start(f32[16,512]{1,0:T(8,128)} %item_ref.3) | copy-start | bytes 98308
  0.6 41.0 %copy-start.4 = (s32[16,4]{0,1:T(4,128)S(1)}, s32[16,4]{0,1:T(4,128)}, u32[]{:S(2)}) copy-start(s32[16,4]{0,1:T(4,128)} %param.7) | copy-start | bytes 772
  0.7 41.0 %copy-start.3 = (s32[16,4]{0,1:T(4,128)S(1)}, s32[16,4]{0,1:T(4,128)}, u32[]{:S(2)}) copy-start(s32[16,4]{0,1:T(4,128)} %param.6) | copy-start | bytes 772
  2.6 39.1 %all-to-all-start = ((bf16[32,8,2048]{2,1,0:T(8,128)(2,1)}), bf16[32,8,2048]{2,1,0:T(8,128)(2,1)S(1)}, u32[]{:S(2)}, u32[]{:S(2)}) async-start(bf16[32,8,2048]{2,1,0:T(8,128)(2,1)} %lower.1), calls=%async_computation | async-start | bytes 2097152 | tf_op jit(solution)/shard_map/all_to_all | solution.py:287
  46.5 24.4 %all-to-all-start.2 = ((bf16[16,16,512]{2,1,0:T(8,128)(2,1)}), bf16[16,16,512]{2,1,0:T(8,128)(2,1)S(1)}, u32[]{:S(2)}, u32[]{:S(2)}) async-start(bf16[16,16,512]{2,1,0:T(8,128)(2,1)} %get-tuple-element.20), calls=%async_computation.2 | async-start | bytes 524288 | tf_op jit(solution)/shard_map/all_to_all | solution.py:287
  57.1 1.6 %copy-start = (bf16[2048,512]{1,0:T(8,128)(2,1)S(1)}, bf16[2048,512]{1,0:T(8,128)(2,1)}, u32[]{:S(2)}) copy-start(bf16[2048,512]{1,0:T(8,128)(2,1)} %get-tuple-element.17.scaled_ref) | copy-start | bytes 6291460
  58.7 19.1 %copy-start.1 = (f32[8,2048]{1,0:T(8,128)S(1)}, f32[8,2048]{1,0:T(8,128)}, u32[]{:S(2)}) copy-start(f32[8,2048]{1,0:T(8,128)} %user_ref.5) | copy-start | bytes 196612
  59.4 10.6 %collective-permute-start = (bf16[16,8,2048]{2,1,0:T(8,128)(2,1)S(1)}, bf16[16,8,2048]{2,1,0:T(8,128)(2,1)S(1)}, u32[]{:S(2)}, u32[]{:S(2)}) collective-permute-start(bf16[16,8,2048]{2,1,0:T(8,128)(2,1)S(1)} %get-tuple-element.19), channel_id=1, source_target_pairs={{0,1},{1,0},{2,3},{3,2},{4,5},{5,4},{6,7},{7,6},{8,9},{9,8},{10,11... | collective-permute-start | bytes 1572872 | tf_op jit(solution)/shard_map/ppermute | solution.py:296
  70.9 16.1 %all-to-all-start.1 = ((bf16[16,8,2048]{2,1,0:T(8,128)(2,1)}), bf16[16,8,2048]{2,1,0:T(8,128)(2,1)S(1)}, u32[]{:S(2)}, u32[]{:S(2)}) async-start(bf16[16,8,2048]{2,1,0:T(8,128)(2,1)} %halves.1), calls=%async_computation.1 | async-start | bytes 1048576 | tf_op jit(solution)/shard_map/all_to_all | solution.py:287
where the time goes:
time: 116 us; the launch traced here: 115 us
  blocking collectives  55.5 us (48%)
  starting transfers between devices  36.9 us (32%)
  waiting for transfers between devices  10.6 us (9%)
  Pallas kernels  9.61 us (8%)
  local copies, waits for them, and re-layouts  1.6 us (1%)
    all_gather x1, blocking collectives, body(): lax.all_gather(item_factor.astype(jnp.bfloat16), 'row', axis=0, tiled=Tru...  28.6 us
    all_to_all x3, starting transfers between devices, exchanged(): lax.all_to_all(blocks, axis, 0, 0, tiled=True, axis_index_groups=groups)  27.8 us
    all_to_all x2, blocking collectives, exchanged(): lax.all_to_all(blocks, axis, 0, 0, tiled=True, axis_index_groups=groups)  26.9 us
    all_to_all x3, waiting for transfers between devices, exchanged(): lax.all_to_all(blocks, axis, 0, 0, tiled=True, axis_index_groups=groups)  9.13 us
    ppermute x1, starting transfers between devices, shifted(): lax.ppermute(array, axis, [(i, (i + by) % count) for i in range(count)])  9.06 us
    pallas_call x1, Pallas kernels, residual_of(): pl.pallas_call(residual_body, in_specs=[FAR] * 5, out_specs=[VMEM] * 3, o...  4.81 us
  transfers between devices with their start and end apart: 4, of which 2 were waited for; matrix products, arithmetic and copies ran while one was open for 0% of the time, Pallas kernels for 2%

commit v1 on v0

--- a/solution.py
+++ b/solution.py
@@ -9,46 +9,54 @@
 TILE = 128
 LANES = 128
 STRIPE = 512
-GATHER_FIRST, SCATTER_FIRST = 0, 9
+GATHER_FIRST, SCATTER_FIRST, SCALARS_FIRST = 9, 1, 9
 COL_LAYER = ("col_0", "col_1", "layer")
 VMEM = pl.BlockSpec(memory_space=pltpu.VMEM)
 SMEM = pl.BlockSpec(memory_space=pltpu.SMEM)
 FAR = pl.BlockSpec(memory_space=pltpu.HBM)
 GRANT = pltpu.CompilerParams(vmem_limit_bytes=16 * 2**20)
-MOST_GRANT = pltpu.CompilerParams(vmem_limit_bytes=52 * 2**20)
-WHOLE_GRANT = pltpu.CompilerParams(vmem_limit_bytes=60 * 2**20)
+MOST_GRANT = pltpu.CompilerParams(vmem_limit_bytes=50 * 2**20)
+LOWER_GRANT = pltpu.CompilerParams(vmem_limit_bytes=60 * 2**20)
 
 epsilon = 1e-12
 trust_ratio = 0.2
 
 
-def lower_body(user_ref, blocks_ref):
-    user = user_ref[...].astype(jnp.bfloat16)
-    blocks_ref[...] = jnp.broadcast_to(user[None], blocks_ref.shape)
-
-
-def lowered_for_all(factor, devices):
+def lower_body(user_ref, item_ref, mask_ref, counts_ref, user_low_ref, item_blocks_ref, limits_ref):
+    item = item_ref[...].astype(jnp.bfloat16)
+    item_blocks_ref[...] = jnp.broadcast_to(item[None], item_blocks_ref.shape)
+    user_low_ref[...] = user_ref[...].astype(jnp.bfloat16)
+    limits_ref[...] = jnp.where(mask_ref[...] == 1, counts_ref[...], 0)
+
+
+def lowered(user_factor, item_factor, mask, counts, devices):
     return pl.pallas_call(
         lower_body,
-        in_specs=[VMEM],
-        out_specs=VMEM,
-        out_shape=jax.ShapeDtypeStruct((devices, *factor.shape), jnp.bfloat16),
-        compiler_params=WHOLE_GRANT,
+        in_specs=[VMEM] * 4,
+        out_specs=[VMEM] * 3,
+        out_shape=[
+            jax.ShapeDtypeStruct(user_factor.shape, jnp.bfloat16),
+            jax.ShapeDtypeStruct((devices, *item_factor.shape), jnp.bfloat16),
+            jax.ShapeDtypeStruct(mask.shape, jnp.int32),
+        ],
+        compiler_params=LOWER_GRANT,
         name="lower",
-    )(factor)
+    )(user_factor, item_factor, mask, counts)
 
 
 def residual_body(
-    far_mask_ref, far_counts_ref, far_user_ref, far_item_ref, far_ratings_ref,
+    layer_ref, far_limits_ref, mine_ref, other_ref, far_item_ref, far_ratings_ref,
     scaled_ref, item_share_ref, error_ref,
-    mask_ref, counts_ref, user_ref, item_ref, ratings_ref, total_ref, sems, ratings_sems,
+    limits_ref, user_ref, item_ref, ratings_ref, total_ref, sems, ratings_sems,
 ):
     columns = ratings_ref.shape[1]
     starts = range(0, ratings_ref.shape[0], STRIPE)
     stripes = [pl.ds(start, STRIPE) for start in starts]
     rank = item_ref.shape[0]
     turn = GATHER_FIRST * rank // 16
-    pairs = [(far_user_ref, user_ref), (far_mask_ref, mask_ref), (far_counts_ref, counts_ref)]
+    layer = layer_ref[0]
+    pairs = [(mine_ref, user_ref.at[:, layer]), (other_ref, user_ref.at[:, 1 - layer])]
+    pairs.append((far_limits_ref, limits_ref))
     pairs.append((far_item_ref.at[pl.ds(0, rank - turn)], item_ref.at[pl.ds(turn, rank - turn)]))
     if turn:
         pairs.append((far_item_ref.at[pl.ds(rank - turn, turn)], item_ref.at[pl.ds(0, turn)]))
@@ -63,14 +71,17 @@
         copy.wait()
     item = item_ref[...]
     side = (TILE, TILE)
+
+    def user_of(at):
+        return user_ref[:, :, :, stripes[at]].reshape(rank, STRIPE)
+
     position = lax.broadcasted_iota(jnp.int32, side, 0) * TILE + lax.broadcasted_iota(jnp.int32, side, 1)
 
     def predicted_of(at):
-        user = user_ref[:, stripes[at]]
-        return lax.dot_general(user, item, (((0,), (0,)), ((), ())), preferred_element_type=jnp.float32)
+        return lax.dot_general(user_of(at), item, (((0,), (0,)), ((), ())), preferred_element_type=jnp.float32)
 
     def add_share(at):
-        share = jnp.dot(user_ref[:, stripes[at]], scaled_ref[stripes[at]], preferred_element_type=jnp.float32)
+        share = jnp.dot(user_of(at), scaled_ref[stripes[at]], preferred_element_type=jnp.float32)
         if at > 0:
             share = share + total_ref[...]
         if at + 1 < len(stripes):
@@ -87,8 +98,7 @@
         following = predicted_of(at + 1) if at + 1 < len(stripes) else None
         for row in range(0, STRIPE, TILE):
             for column in range(0, columns, TILE):
-                tile_at = (column // TILE, (start + row) // TILE)
-                limit = jnp.where(mask_ref[tile_at] == 1, counts_ref[tile_at], 0)
+                limit = limits_ref[column // TILE, (start + row) // TILE]
                 rows, cols = pl.ds(start + row, TILE), pl.ds(column, TILE)
                 rating = ratings_ref[rows, cols].astype(jnp.float32)
                 difference = predicted[row : row + TILE, column : column + TILE] - rating
@@ -103,12 +113,12 @@
     error_ref[...] = jnp.concatenate(errors, axis=1)
 
 
-def residual_of(mask, counts, user, item, ratings, devices):
+def residual_of(layer, limits, mine, other, item, ratings, devices):
     rank, columns = item.shape
     flops = 4 * rank * ratings.size
     return pl.pallas_call(
         residual_body,
-        in_specs=[FAR] * 5,
+        in_specs=[SMEM] + [FAR] * 5,
         out_specs=[VMEM] * 3,
         out_shape=[
             jax.ShapeDtypeStruct(ratings.shape, jnp.bfloat16),
@@ -116,9 +126,8 @@
             jax.ShapeDtypeStruct((8, columns), jnp.float32),
         ],
         scratch_shapes=[
-            pltpu.SMEM(mask.shape, jnp.int32),
-            pltpu.SMEM(counts.shape, jnp.int32),
-            pltpu.VMEM(user.shape, jnp.bfloat16),
+            pltpu.SMEM(limits.shape, jnp.int32),
+            pltpu.VMEM((mine.shape[0], 2, *mine.shape[1:]), jnp.bfloat16),
             pltpu.VMEM(item.shape, jnp.bfloat16),
             pltpu.VMEM(ratings.shape, jnp.bfloat16),
             pltpu.VMEM((rank, columns), jnp.float32),
@@ -128,15 +137,22 @@
         cost_estimate=pl.CostEstimate(flops=flops, bytes_accessed=4 * ratings.size, transcendentals=0),
         compiler_params=MOST_GRANT,
         name="residual",
-    )(mask, counts, user, item, ratings)
-
-
-def user_share_body(layer_ref, item_ref, scaled_ref, mine_ref, other_ref):
+    )(layer, limits, mine, other, item, ratings)
+
+
+def user_share_body(layer_ref, item_ref, far_scaled_ref, mine_ref, other_ref, scaled_ref, sems):
     chips, height, _ = mine_ref.shape
+    stripes = [pl.ds(start, STRIPE) for start in range(0, scaled_ref.shape[0], STRIPE)]
+    copies = [
+        pltpu.make_async_copy(far_scaled_ref.at[stripe], scaled_ref.at[stripe], sems.at[at])
+        for at, stripe in enumerate(stripes)
+    ]
+    for copy in copies:
+        copy.start()
     item = item_ref[...]
     first = layer_ref[0] == 0
-    for start in range(0, scaled_ref.shape[0], STRIPE):
-        stripe = pl.ds(start, STRIPE)
+    for stripe, copy in zip(stripes, copies):
+        copy.wait()
         share = lax.dot_general(item, scaled_ref[stripe], (((1,), (1,)), ((), ())), preferred_element_type=jnp.float32)
         share = share.reshape(chips, 2, height, STRIPE)
         for at in range(chips):
@@ -150,11 +166,15 @@
     shape = jax.ShapeDtypeStruct((item.shape[0] // height // 2, height, scaled.shape[0]), jnp.bfloat16)
     return pl.pallas_call(
         user_share_body,
-        in_specs=[SMEM, VMEM, VMEM],
+        in_specs=[SMEM, VMEM, FAR],
         out_specs=[VMEM, VMEM],
         out_shape=[shape, shape],
+        scratch_shapes=[
+            pltpu.VMEM(scaled.shape, jnp.bfloat16),
+            pltpu.SemaphoreType.DMA((scaled.shape[0] // STRIPE,)),
+        ],
         cost_estimate=pl.CostEstimate(flops=2 * item.shape[0] * scaled.size, bytes_accessed=0, transcendentals=0),
-        compiler_params=GRANT,
+        compiler_params=MOST_GRANT,
         name="user_share",
     )(layer, item, scaled)
 
@@ -181,7 +201,7 @@
     return total
 
 
-def item_raw_body(mask_ref, counts_ref, arrived_ref, user_ref, item_ref, error_ref, raw_ref, sums_ref):
+def item_raw_body(limits_ref, arrived_ref, user_ref, item_ref, error_ref, raw_ref, sums_ref):
     raw = summed(arrived_ref)
     raw_ref[...] = raw
     user, item = user_ref[...], item_ref[...]
@@ -189,7 +209,7 @@
     sums = jnp.zeros(sums_ref.shape, jnp.float32)
     for at, value in enumerate(
         (
-            jnp.sum((mask_ref[...] * counts_ref[...]).astype(jnp.float32)),
+            jnp.sum(limits_ref[...].astype(jnp.float32)),
             jnp.sum(user * user) + jnp.sum(item * item),
             jnp.sum(error_ref[...]),
             jnp.sum(raw * raw),
@@ -199,10 +219,10 @@
     sums_ref[...] = sums
 
 
-def item_raw_of(mask, counts, arrived, user_factor, item_factor, error):
+def item_raw_of(limits, arrived, user_factor, item_factor, error):
     return pl.pallas_call(
         item_raw_body,
-        in_specs=[VMEM] * 6,
+        in_specs=[VMEM] * 5,
         out_specs=[VMEM, VMEM],
         out_shape=[
             jax.ShapeDtypeStruct(arrived.shape[1:], jnp.float32),
@@ -210,7 +230,7 @@
         ],
         compiler_params=GRANT,
         name="item_raw",
-    )(mask, counts, arrived, user_factor, item_factor, error)
+    )(limits, arrived, user_factor, item_factor, error)
 
 
 def user_raw_body(arrived_ref, sums_ref, raw_ref, packed_ref):
@@ -298,23 +318,27 @@
 
 def body(ratings, tile_mask, tile_counts, user_factor, item_factor):
     rows, height = lax.axis_size("row"), user_factor.shape[0]
-    gather_list, scatter_list = (listed_from(first * rows // 16, rows) for first in (GATHER_FIRST, SCATTER_FIRST))
+    gather_list, scatter_list, scalars_list = (
+        listed_from(first * rows // 16, rows) for first in (GATHER_FIRST, SCATTER_FIRST, SCALARS_FIRST)
+    )
     layer = lax.axis_index("layer").astype(jnp.int32)[None]
     mask, counts = tile_mask.T, tile_counts.T
-    user = exchanged(lowered_for_all(user_factor, lax.axis_size(COL_LAYER)), COL_LAYER)
-    user = user.reshape(-1, user_factor.shape[1])
-    item = lax.all_gather(item_factor.astype(jnp.bfloat16), "row", axis=0, tiled=True, axis_index_groups=gather_list)
-    scaled, item_share, error = residual_of(mask, counts, user, item, ratings, rows)
+    user_low, item_blocks, limits = lowered(user_factor, item_factor, mask, counts, rows)
+    item = exchanged(item_blocks, "row", gather_list).reshape(-1, item_factor.shape[1])
+    mine = lax.all_gather(user_low, ("col_0", "col_1"), axis=0, tiled=True)
+    mine = mine.reshape(-1, *user_factor.shape)
+    other = shifted(mine, "layer", 1)
+    scaled, item_share, error = residual_of(layer, limits, mine, other, item, ratings, rows)
     item_arrived = exchanged(item_share, "row", scatter_list)
     my_share, other_share = user_share_of(layer, item, scaled, height)
     partner_share = shifted(other_share, "layer", 1)
     halves = halves_summed(my_share, partner_share)
     user_arrived = exchanged(halves, ("col_0", "col_1"))
-    raw_item, sums = item_raw_of(mask, counts, item_arrived, user_factor, item_factor, error)
+    raw_item, sums = item_raw_of(limits, item_arrived, user_factor, item_factor, error)
     raw_user, packed = user_raw_of(user_arrived, sums, lax.axis_size(COL_LAYER))
     packed = exchanged(packed, COL_LAYER)
     packed = packed_again(packed, rows)
-    packed = exchanged(packed, "row", scatter_list)
+    packed = exchanged(packed, "row", scalars_list)
     new_user, new_item, loss_value, grad_norm = stepped(packed, user_factor, item_factor, raw_user, raw_item)
     return (new_user, new_item, loss_value.reshape(()), grad_norm.reshape(()))
 

time: 116 us -> 120 us (1.034)
  waiting for transfers between devices: 10.6 us -> 24.7 us
  blocking collectives: 55.5 us -> 46.4 us
    all_to_all x3, waiting for transfers between devices: 9.13 us -> 21.7 us  [exchanged(): lax.all_to_all(blocks, axis, 0, 0, tiled=True, axis_index_groups=groups)]
    all_gather x1, blocking collectives: 28.6 us -> 20.1 us  [body(): mine = lax.all_gather(user_low, ('col_0', 'col_1'), axis=0, tiled=True)]
    ppermute x1 -> x2, waiting for transfers between devices: 1.51 us -> 3.03 us  [shifted(): lax.ppermute(array, axis, [(i, (i + by) % count) for i in range(count)])]
    ppermute x1 -> x2, starting transfers between devices: 9.06 us -> 9.9 us  [shifted(): lax.ppermute(array, axis, [(i, (i + by) % count) for i in range(count)])]
  transfers between devices with their start and end apart: 4 -> 5, of which waited for: 2 -> 4; matrix products, arithmetic and copies ran while one was open for 0% -> 0% of each run, Pallas kernels for 2% -> 2%
where the time goes in v1:
time: 120 us
  blocking collectives  46.4 us (39%)
  starting transfers between devices  37.3 us (31%)
  waiting for transfers between devices  24.7 us (21%)
  Pallas kernels  9.86 us (8%)
    all_to_all x3, starting transfers between devices, exchanged(): lax.all_to_all(blocks, axis, 0, 0, tiled=True, axis_index_groups=groups)  27.4 us
    all_to_all x2, blocking collectives, exchanged(): lax.all_to_all(blocks, axis, 0, 0, tiled=True, axis_index_groups=groups)  26.2 us
    all_to_all x3, waiting for transfers between devices, exchanged(): lax.all_to_all(blocks, axis, 0, 0, tiled=True, axis_index_groups=groups)  21.7 us
    all_gather x1, blocking collectives, body(): mine = lax.all_gather(user_low, ('col_0', 'col_1'), axis=0, tiled=True)  20.1 us
    ppermute x2, starting transfers between devices, shifted(): lax.ppermute(array, axis, [(i, (i + by) % count) for i in range(count)])  9.9 us
    pallas_call x1, Pallas kernels, residual_of(): pl.pallas_call(residual_body, in_specs=[SMEM] + [FAR] * 5, out_specs=[VME...  4.63 us
    ppermute x2, waiting for transfers between devices, shifted(): lax.ppermute(array, axis, [(i, (i + by) % count) for i in range(count)])  3.03 us
  transfers between devices with their start and end apart: 5, of which 4 were waited for; matrix products, arithmetic and copies ran while one was open for 0% of the time, Pallas kernels for 2%

profile of v1, /device:TPU:1, one launch (start us, length us, event | category | flops | bytes accessed | tf_op | source)
XLA Modules:
  0.0 119.7 jit_solution(3279101638076122878)
XLA Ops:
  0.6 1.6 %lower.1 = (bf16[8,2048]{1,0:T(8,128)(2,1)}, bf16[16,16,512]{2,1,0:T(8,128)(2,1)}, s32[4,16]{1,0:T(4,128)}) custom-call(f32[8,2048]{1,0:T(8,128)} %user_ref.5, f32[16,512]{1,0:T(8,128)} %item_ref.5, s32[4,16]{1,0:T(4,128)} %bitcast.11, s32[4,16]{1,0:T(4,128)} %bitcast.12), custom_call_target="tpu_custom_call" | custom-call | tf_op jit(solution)/shard_map/lower/pallas_call | solution.py:33
  2.2 18.2 %all-to-all-start = ((bf16[16,16,512]{2,1,0:T(8,128)(2,1)}), bf16[16,16,512]{2,1,0:T(8,128)(2,1)S(1)}, u32[]{:S(2)}, u32[]{:S(2)}) async-start(bf16[16,16,512]{2,1,0:T(8,128)(2,1)} %get-tuple-element.20), calls=%async_computation | async-start | bytes 524288 | tf_op jit(solution)/shard_map/all_to_all | solution.py:307
  20.4 20.1 %all_gather.3 = bf16[128,2048]{1,0:T(8,128)(2,1)S(1)} all-gather(bf16[8,2048]{1,0:T(8,128)(2,1)} %get-tuple-element.22), channel_id=1, replica_groups=mesh['row'=16,'col_0'=4,'col_1'=4,'layer'=2] {'col_0','col_1'}, dimensions={0}, use_global_device_ids=true | all-gather | bytes 557056 | tf_op jit(solution)/shard_map/all_gather | solution.py:328
  40.6 7.3 %collective-permute-start = (bf16[16,8,2048]{2,1,0:T(8,128)(2,1)S(1)}, bf16[16,8,2048]{2,1,0:T(8,128)(2,1)S(1)}, u32[]{:S(2)}, u32[]{:S(2)}) collective-permute-start(bf16[16,8,2048]{2,1,0:T(8,128)(2,1)S(1)} %bitcast.9), channel_id=1, source_target_pairs={{0,1},{1,0},{2,3},{3,2},{4,5},{5,4},{6,7},{7,6},{8,9},{9,8},{10,11... | collective-permute-start | bytes 1572872 | tf_op jit(solution)/shard_map/ppermute | solution.py:316
  47.9 1.5 %collective-permute-done.other_ref = bf16[16,8,2048]{2,1,0:T(8,128)(2,1)S(1)} collective-permute-done((bf16[16,8,2048]{2,1,0:T(8,128)(2,1)S(1)}, bf16[16,8,2048]{2,1,0:T(8,128)(2,1)S(1)}, u32[]{:S(2)}, u32[]{:S(2)}) %collective-permute-start) | collective-permute-done | bytes 524320 | tf_op jit(solution)/shard_map/ppermute | solution.py:316
  49.4 0.0 all-to-all-done
  49.5 0.0 copy-start.2
  49.5 0.7 copy-done.2
  50.1 4.6 %residual.1 = (bf16[2048,512]{1,0:T(8,128)(2,1)S(1)}, bf16[16,16,512]{2,1,0:T(8,128)(2,1)}, f32[8,512]{1,0:T(8,128)S(1)}) custom-call(s32[1]{0:T(128)} %bitcast.layer_ref, s32[4,16]{1,0:T(4,128)S(1)} %copy-done.2, bf16[16,8,2048]{2,1,0:T(8,128)(2,1)S(1)} %bitcast.10, bf16[16,8,2048]{2,1,0:T(8,128)(2,1)S(1)} %collective-permute-done.other_ref, ...), custom_call_target="tpu_custom_call" | custom-call | flops 1073741824 | bytes 4194304 | tf_op jit(solution)/shard_map/residual/pallas_call | solution.py:119
  54.8 4.6 %all-to-all-start.2 = ((bf16[16,16,512]{2,1,0:T(8,128)(2,1)}), bf16[16,16,512]{2,1,0:T(8,128)(2,1)S(1)}, u32[]{:S(2)}, u32[]{:S(2)}) async-start(bf16[16,16,512]{2,1,0:T(8,128)(2,1)} %get-tuple-element.26), calls=%async_computation.2 | async-start | bytes 524288 | tf_op jit(solution)/shard_map/all_to_all | solution.py:307
  59.4 0.0 copy-start
  59.4 0.0 copy-start.1
  59.4 0.0 copy-start.3
  59.4 1.5 %user_share.1 = (bf16[16,8,2048]{2,1,0:T(8,128)(2,1)S(1)}, bf16[16,8,2048]{2,1,0:T(8,128)(2,1)S(1)}) custom-call(s32[1]{0:T(128)} %bitcast.layer_ref, bf16[256,512]{1,0:T(8,128)(2,1)S(1)} %bitcast.8, bf16[2048,512]{1,0:T(8,128)(2,1)S(1)} %get-tuple-element.23.far_scaled_ref), custom_call_target="tpu_custom_call" | custom-call | flops 536870912 | tf_op jit(solution)/shard_map/user_share/pallas_call | solution.py:167
  61.0 2.6 %collective-permute-start.1 = (bf16[16,8,2048]{2,1,0:T(8,128)(2,1)S(1)}, bf16[16,8,2048]{2,1,0:T(8,128)(2,1)S(1)}, u32[]{:S(2)}, u32[]{:S(2)}) collective-permute-start(bf16[16,8,2048]{2,1,0:T(8,128)(2,1)S(1)} %get-tuple-element.25), channel_id=1, source_target_pairs={{0,1},{1,0},{2,3},{3,2},{4,5},{5,4},{6,7},{7,6},{8,9},{9,8},{10,11... | collective-permute-start | bytes 1572872 | tf_op jit(solution)/shard_map/ppermute | solution.py:316
  63.5 1.5 %collective-permute-done.1.arrived_ref = bf16[16,8,2048]{2,1,0:T(8,128)(2,1)S(1)} collective-permute-done((bf16[16,8,2048]{2,1,0:T(8,128)(2,1)S(1)}, bf16[16,8,2048]{2,1,0:T(8,128)(2,1)S(1)}, u32[]{:S(2)}, u32[]{:S(2)}) %collective-permute-start.1) | collective-permute-done | bytes 524320 | tf_op jit(solution)/shard_map/ppermute | solution.py:316
  65.0 0.9 halves.1
  66.0 12.6 %all-to-all-done.2.arrived_ref = bf16[16,16,512]{2,1,0:T(8,128)(2,1)S(1)} async-done(((bf16[16,16,512]{2,1,0:T(8,128)(2,1)}), bf16[16,16,512]{2,1,0:T(8,128)(2,1)S(1)}, u32[]{:S(2)}, u32[]{:S(2)}) %all-to-all-start.2) | async-done | bytes 262176 | tf_op jit(solution)/shard_map/all_to_all | solution.py:307
  78.6 4.6 %all-to-all-start.1 = ((bf16[16,8,2048]{2,1,0:T(8,128)(2,1)}), bf16[16,8,2048]{2,1,0:T(8,128)(2,1)S(1)}, u32[]{:S(2)}, u32[]{:S(2)}) async-start(bf16[16,8,2048]{2,1,0:T(8,128)(2,1)} %halves.1), calls=%async_computation.1 | async-start | bytes 1048576 | tf_op jit(solution)/shard_map/all_to_all | solution.py:307
  83.2 0.0 copy-done
  83.2 0.0 copy-done.1
  83.2 0.0 copy-done.3
  83.2 0.2 item_raw.1
  83.4 9.1 %all-to-all-done.1.arrived_ref = bf16[16,8,2048]{2,1,0:T(8,128)(2,1)S(1)} async-done(((bf16[16,8,2048]{2,1,0:T(8,128)(2,1)}), bf16[16,8,2048]{2,1,0:T(8,128)(2,1)S(1)}, u32[]{:S(2)}, u32[]{:S(2)}) %all-to-all-start.1) | async-done | bytes 524320 | tf_op jit(solution)/shard_map/all_to_all | solution.py:307
  92.5 0.2 user_raw.1
  92.7 13.4 %all_to_all.25.arrived_ref = f32[32,1,128]{2,1,0:T(1,128)S(1)} all-to-all(f32[32,1,128]{2,1,0:T(1,128)S(1)} %get-tuple-element.29), channel_id=1, replica_groups=mesh['row'=16,'col_0'=4,'col_1'=4,'layer'=2] {'col_0','col_1','layer'}, dimensions={0} | all-to-all | bytes 32768 | tf_op jit(solution)/shard_map/all_to_all | solution.py:307
  106.1 12.9 %all_to_all.26.arrived_ref = f32[16,1,128]{2,1,0:T(1,128)S(1)} all-to-all(f32[16,1,128]{2,1,0:T(1,128)S(1)} %packed_again.1), channel_id=1, replica_groups={{288,320,352,384,416,448,480,0,32,64,96,128,160,192,224,256},{289,321,3..., dimensions={0} | all-to-all | bytes 16384 | tf_op jit(solution)/shard_map/all_to_all | solution.py:307
  119.0 0.8 step.1
  (1 shorter events, 0.0 us)
Async XLA Ops:
  2.2 47.2 %all-to-all-start = ((bf16[16,16,512]{2,1,0:T(8,128)(2,1)}), bf16[16,16,512]{2,1,0:T(8,128)(2,1)S(1)}, u32[]{:S(2)}, u32[]{:S(2)}) async-start(bf16[16,16,512]{2,1,0:T(8,128)(2,1)} %get-tuple-element.20), calls=%async_computation | async-start | bytes 524288 | tf_op jit(solution)/shard_map/all_to_all | solution.py:307
  40.6 8.9 %collective-permute-start = (bf16[16,8,2048]{2,1,0:T(8,128)(2,1)S(1)}, bf16[16,8,2048]{2,1,0:T(8,128)(2,1)S(1)}, u32[]{:S(2)}, u32[]{:S(2)}) collective-permute-start(bf16[16,8,2048]{2,1,0:T(8,128)(2,1)S(1)} %bitcast.9), channel_id=1, source_target_pairs={{0,1},{1,0},{2,3},{3,2},{4,5},{5,4},{6,7},{7,6},{8,9},{9,8},{10,11... | collective-permute-start | bytes 1572872 | tf_op jit(solution)/shard_map/ppermute | solution.py:316
  49.5 0.7 copy-start.2
  54.8 23.8 %all-to-all-start.2 = ((bf16[16,16,512]{2,1,0:T(8,128)(2,1)}), bf16[16,16,512]{2,1,0:T(8,128)(2,1)S(1)}, u32[]{:S(2)}, u32[]{:S(2)}) async-start(bf16[16,16,512]{2,1,0:T(8,128)(2,1)} %get-tuple-element.26), calls=%async_computation.2 | async-start | bytes 524288 | tf_op jit(solution)/shard_map/all_to_all | solution.py:307
  59.4 23.8 %copy-start = (f32[8,2048]{1,0:T(8,128)S(1)}, f32[8,2048]{1,0:T(8,128)}, u32[]{:S(2)}) copy-start(f32[8,2048]{1,0:T(8,128)} %user_ref.5) | copy-start | bytes 196612
  59.4 23.8 %copy-start.1 = (f32[16,512]{1,0:T(8,128)S(1)}, f32[16,512]{1,0:T(8,128)}, u32[]{:S(2)}) copy-start(f32[16,512]{1,0:T(8,128)} %item_ref.5) | copy-start | bytes 98308
  59.4 23.8 %copy-start.3 = (s32[4,16]{1,0:T(4,128)S(1)}, s32[4,16]{1,0:T(4,128)}, u32[]{:S(2)}) copy-start(s32[4,16]{1,0:T(4,128)} %get-tuple-element.21.far_limits_ref.limits_ref) | copy-start | bytes 772
  61.0 4.1 %collective-permute-start.1 = (bf16[16,8,2048]{2,1,0:T(8,128)(2,1)S(1)}, bf16[16,8,2048]{2,1,0:T(8,128)(2,1)S(1)}, u32[]{:S(2)}, u32[]{:S(2)}) collective-permute-start(bf16[16,8,2048]{2,1,0:T(8,128)(2,1)S(1)} %get-tuple-element.25), channel_id=1, source_target_pairs={{0,1},{1,0},{2,3},{3,2},{4,5},{5,4},{6,7},{7,6},{8,9},{9,8},{10,11... | collective-permute-start | bytes 1572872 | tf_op jit(solution)/shard_map/ppermute | solution.py:316
  78.6 13.9 %all-to-all-start.1 = ((bf16[16,8,2048]{2,1,0:T(8,128)(2,1)}), bf16[16,8,2048]{2,1,0:T(8,128)(2,1)S(1)}, u32[]{:S(2)}, u32[]{:S(2)}) async-start(bf16[16,8,2048]{2,1,0:T(8,128)(2,1)} %halves.1), calls=%async_computation.1 | async-start | bytes 1048576 | tf_op jit(solution)/shard_map/all_to_all | solution.py:307

commit v2 on v1

--- a/solution.py
+++ b/solution.py
@@ -9,37 +9,36 @@
 TILE = 128
 LANES = 128
 STRIPE = 512
-GATHER_FIRST, SCATTER_FIRST, SCALARS_FIRST = 9, 1, 9
+GATHER_FIRST, SCATTER_FIRST, SCALARS_FIRST, CHIP_FIRST = 9, 9, 8, 15
 COL_LAYER = ("col_0", "col_1", "layer")
 VMEM = pl.BlockSpec(memory_space=pltpu.VMEM)
 SMEM = pl.BlockSpec(memory_space=pltpu.SMEM)
 FAR = pl.BlockSpec(memory_space=pltpu.HBM)
 GRANT = pltpu.CompilerParams(vmem_limit_bytes=16 * 2**20)
 MOST_GRANT = pltpu.CompilerParams(vmem_limit_bytes=50 * 2**20)
-LOWER_GRANT = pltpu.CompilerParams(vmem_limit_bytes=60 * 2**20)
+WHOLE_GRANT = pltpu.CompilerParams(vmem_limit_bytes=60 * 2**20)
 
 epsilon = 1e-12
 trust_ratio = 0.2
 
 
-def lower_body(user_ref, item_ref, mask_ref, counts_ref, user_low_ref, item_blocks_ref, limits_ref):
-    item = item_ref[...].astype(jnp.bfloat16)
-    item_blocks_ref[...] = jnp.broadcast_to(item[None], item_blocks_ref.shape)
-    user_low_ref[...] = user_ref[...].astype(jnp.bfloat16)
+def lower_body(user_ref, item_ref, mask_ref, counts_ref, user_blocks_ref, item_blocks_ref, limits_ref):
+    user_blocks_ref[...] = jnp.broadcast_to(user_ref[...].astype(jnp.bfloat16)[None], user_blocks_ref.shape)
+    item_blocks_ref[...] = jnp.broadcast_to(item_ref[...].astype(jnp.bfloat16)[None], item_blocks_ref.shape)
     limits_ref[...] = jnp.where(mask_ref[...] == 1, counts_ref[...], 0)
 
 
-def lowered(user_factor, item_factor, mask, counts, devices):
+def lowered(user_factor, item_factor, mask, counts, chips, rows):
     return pl.pallas_call(
         lower_body,
         in_specs=[VMEM] * 4,
         out_specs=[VMEM] * 3,
         out_shape=[
-            jax.ShapeDtypeStruct(user_factor.shape, jnp.bfloat16),
-            jax.ShapeDtypeStruct((devices, *item_factor.shape), jnp.bfloat16),
+            jax.ShapeDtypeStruct((chips, *user_factor.shape), jnp.bfloat16),
+            jax.ShapeDtypeStruct((rows, *item_factor.shape), jnp.bfloat16),
             jax.ShapeDtypeStruct(mask.shape, jnp.int32),
         ],
-        compiler_params=LOWER_GRANT,
+        compiler_params=WHOLE_GRANT,
         name="lower",
     )(user_factor, item_factor, mask, counts)
 
@@ -52,14 +51,19 @@
     columns = ratings_ref.shape[1]
     starts = range(0, ratings_ref.shape[0], STRIPE)
     stripes = [pl.ds(start, STRIPE) for start in starts]
-    rank = item_ref.shape[0]
+    layer, chips, (rank, _) = layer_ref[0], mine_ref.shape[0], item_ref.shape
     turn = GATHER_FIRST * rank // 16
-    layer = layer_ref[0]
-    pairs = [(mine_ref, user_ref.at[:, layer]), (other_ref, user_ref.at[:, 1 - layer])]
-    pairs.append((far_limits_ref, limits_ref))
-    pairs.append((far_item_ref.at[pl.ds(0, rank - turn)], item_ref.at[pl.ds(turn, rank - turn)]))
-    if turn:
-        pairs.append((far_item_ref.at[pl.ds(rank - turn, turn)], item_ref.at[pl.ds(0, turn)]))
+    pairs = [
+        (far_limits_ref, limits_ref),
+        (far_item_ref.at[pl.ds(0, rank - turn)], item_ref.at[pl.ds(turn, rank - turn)]),
+        (far_item_ref.at[pl.ds(rank - turn, turn)], item_ref.at[pl.ds(0, turn)]),
+    ]
+    turn = CHIP_FIRST * chips // 16
+    for half_ref, core in ((mine_ref, layer), (other_ref, 1 - layer)):
+        pairs += [
+            (half_ref.at[pl.ds(0, chips - turn)], user_ref.at[pl.ds(turn, chips - turn), core]),
+            (half_ref.at[pl.ds(chips - turn, turn)], user_ref.at[pl.ds(0, turn), core]),
+        ]
     copies = [pltpu.make_async_copy(far, near, sems.at[at]) for at, (far, near) in enumerate(pairs)]
     ratings_copies = [
         pltpu.make_async_copy(far_ratings_ref.at[stripe], ratings_ref.at[stripe], ratings_sems.at[at])
@@ -131,7 +135,7 @@
             pltpu.VMEM(item.shape, jnp.bfloat16),
             pltpu.VMEM(ratings.shape, jnp.bfloat16),
             pltpu.VMEM((rank, columns), jnp.float32),
-            pltpu.SemaphoreType.DMA((5,)),
+            pltpu.SemaphoreType.DMA((7,)),
             pltpu.SemaphoreType.DMA((ratings.shape[0] // STRIPE,)),
         ],
         cost_estimate=pl.CostEstimate(flops=flops, bytes_accessed=4 * ratings.size, transcendentals=0),
@@ -140,24 +144,17 @@
     )(layer, limits, mine, other, item, ratings)
 
 
-def user_share_body(layer_ref, item_ref, far_scaled_ref, mine_ref, other_ref, scaled_ref, sems):
+def user_share_body(layer_ref, item_ref, scaled_ref, mine_ref, other_ref):
     chips, height, _ = mine_ref.shape
-    stripes = [pl.ds(start, STRIPE) for start in range(0, scaled_ref.shape[0], STRIPE)]
-    copies = [
-        pltpu.make_async_copy(far_scaled_ref.at[stripe], scaled_ref.at[stripe], sems.at[at])
-        for at, stripe in enumerate(stripes)
-    ]
-    for copy in copies:
-        copy.start()
     item = item_ref[...]
     first = layer_ref[0] == 0
-    for stripe, copy in zip(stripes, copies):
-        copy.wait()
+    for start in range(0, scaled_ref.shape[0], STRIPE):
+        stripe = pl.ds(start, STRIPE)
         share = lax.dot_general(item, scaled_ref[stripe], (((1,), (1,)), ((), ())), preferred_element_type=jnp.float32)
         share = share.reshape(chips, 2, height, STRIPE)
         for at in range(chips):
             even, odd = share[at, 0], share[at, 1]
-            chip = (at + GATHER_FIRST * chips // 16) % chips
+            chip = (at + (GATHER_FIRST - CHIP_FIRST) * chips // 16) % chips
             mine_ref[chip, :, stripe] = jnp.where(first, even, odd).astype(jnp.bfloat16)
             other_ref[chip, :, stripe] = jnp.where(first, odd, even).astype(jnp.bfloat16)
 
@@ -166,15 +163,11 @@
     shape = jax.ShapeDtypeStruct((item.shape[0] // height // 2, height, scaled.shape[0]), jnp.bfloat16)
     return pl.pallas_call(
         user_share_body,
-        in_specs=[SMEM, VMEM, FAR],
+        in_specs=[SMEM, VMEM, VMEM],
         out_specs=[VMEM, VMEM],
         out_shape=[shape, shape],
-        scratch_shapes=[
-            pltpu.VMEM(scaled.shape, jnp.bfloat16),
-            pltpu.SemaphoreType.DMA((scaled.shape[0] // STRIPE,)),
-        ],
         cost_estimate=pl.CostEstimate(flops=2 * item.shape[0] * scaled.size, bytes_accessed=0, transcendentals=0),
-        compiler_params=MOST_GRANT,
+        compiler_params=GRANT,
         name="user_share",
     )(layer, item, scaled)
 
@@ -318,25 +311,27 @@
 
 def body(ratings, tile_mask, tile_counts, user_factor, item_factor):
     rows, height = lax.axis_size("row"), user_factor.shape[0]
+    devices, chips = lax.axis_size(COL_LAYER), lax.axis_size(("col_0", "col_1"))
     gather_list, scatter_list, scalars_list = (
         listed_from(first * rows // 16, rows) for first in (GATHER_FIRST, SCATTER_FIRST, SCALARS_FIRST)
     )
+    chips_list, devices_list = (listed_from(CHIP_FIRST * count // 16, count) for count in (chips, devices))
     layer = lax.axis_index("layer").astype(jnp.int32)[None]
-    mask, counts = tile_mask.T, tile_counts.T
-    user_low, item_blocks, limits = lowered(user_factor, item_factor, mask, counts, rows)
+    user_blocks, item_blocks, limits = lowered(
+        user_factor, item_factor, tile_mask.T, tile_counts.T, chips, rows
+    )
+    mine = exchanged(user_blocks, ("col_0", "col_1"), chips_list)
     item = exchanged(item_blocks, "row", gather_list).reshape(-1, item_factor.shape[1])
-    mine = lax.all_gather(user_low, ("col_0", "col_1"), axis=0, tiled=True)
-    mine = mine.reshape(-1, *user_factor.shape)
     other = shifted(mine, "layer", 1)
     scaled, item_share, error = residual_of(layer, limits, mine, other, item, ratings, rows)
     item_arrived = exchanged(item_share, "row", scatter_list)
     my_share, other_share = user_share_of(layer, item, scaled, height)
     partner_share = shifted(other_share, "layer", 1)
     halves = halves_summed(my_share, partner_share)
-    user_arrived = exchanged(halves, ("col_0", "col_1"))
+    user_arrived = exchanged(halves, ("col_0", "col_1"), chips_list)
     raw_item, sums = item_raw_of(limits, item_arrived, user_factor, item_factor, error)
-    raw_user, packed = user_raw_of(user_arrived, sums, lax.axis_size(COL_LAYER))
-    packed = exchanged(packed, COL_LAYER)
+    raw_user, packed = user_raw_of(user_arrived, sums, devices)
+    packed = exchanged(packed, COL_LAYER, devices_list)
     packed = packed_again(packed, rows)
     packed = exchanged(packed, "row", scalars_list)
     new_user, new_item, loss_value, grad_norm = stepped(packed, user_factor, item_factor, raw_user, raw_item)

time: 120 us -> 121 us (level)
  starting transfers between devices: 37.3 us -> 45.6 us
  blocking collectives: 46.4 us -> 39.4 us
    all_gather x1 -> x0, blocking collectives: 20.1 us -> none  [body(): mine = lax.all_gather(user_low, ('col_0', 'col_1'), axis=0, tiled=True)]
    all_to_all x2 -> x3, blocking collectives: 26.2 us -> 39.4 us  [exchanged(): lax.all_to_all(blocks, axis, 0, 0, tiled=True, axis_index_groups=groups)]
    all_to_all x3, starting transfers between devices: 27.4 us -> 37.8 us  [exchanged(): lax.all_to_all(blocks, axis, 0, 0, tiled=True, axis_index_groups=groups)]
    ppermute x2, starting transfers between devices: 9.9 us -> 7.74 us  [shifted(): lax.ppermute(array, axis, [(i, (i + by) % count) for i in range(count)])]
    ppermute x2, waiting for transfers between devices: 3.03 us -> 1.52 us  [shifted(): lax.ppermute(array, axis, [(i, (i + by) % count) for i in range(count)])]
    all_to_all x3, waiting for transfers between devices: 21.7 us -> 23 us  [exchanged(): lax.all_to_all(blocks, axis, 0, 0, tiled=True, axis_index_groups=groups)]
where the time goes in v2:
time: 121 us; the launch traced here: 120 us
  starting transfers between devices  45.6 us (38%)
  blocking collectives  39.4 us (33%)
  waiting for transfers between devices  24.6 us (20%)
  Pallas kernels  9.3 us (8%)
    all_to_all x3, blocking collectives, exchanged(): lax.all_to_all(blocks, axis, 0, 0, tiled=True, axis_index_groups=groups)  39.4 us
    all_to_all x3, starting transfers between devices, exchanged(): lax.all_to_all(blocks, axis, 0, 0, tiled=True, axis_index_groups=groups)  37.8 us
    all_to_all x3, waiting for transfers between devices, exchanged(): lax.all_to_all(blocks, axis, 0, 0, tiled=True, axis_index_groups=groups)  23 us
    ppermute x2, starting transfers between devices, shifted(): lax.ppermute(array, axis, [(i, (i + by) % count) for i in range(count)])  7.74 us
    pallas_call x1, Pallas kernels, residual_of(): pl.pallas_call(residual_body, in_specs=[SMEM] + [FAR] * 5, out_specs=[VME...  4.69 us
  transfers between devices with their start and end apart: 5, of which 4 were waited for; matrix products, arithmetic and copies ran while one was open for 0% of the time, Pallas kernels for 2%

profile of v2, /device:TPU:1, one launch (start us, length us, event | category | flops | bytes accessed | tf_op | source)
XLA Modules:
  0.0 120.2 jit_solution(12247329053652481316)
XLA Ops:
  0.6 1.8 %lower.1 = (bf16[16,8,2048]{2,1,0:T(8,128)(2,1)}, bf16[16,16,512]{2,1,0:T(8,128)(2,1)}, s32[4,16]{1,0:T(4,128)}) custom-call(f32[8,2048]{1,0:T(8,128)} %user_ref.5, f32[16,512]{1,0:T(8,128)} %item_ref.5, s32[4,16]{1,0:T(4,128)} %bitcast.8, s32[4,16]{1,0:T(4,128)} %bitcast.9), custom_call_target="tpu_custom_call" | custom-call | tf_op jit(solution)/shard_map/lower/pallas_call | solution.py:32
  2.4 14.4 %all_to_all.30.mine_ref = bf16[16,8,2048]{2,1,0:T(8,128)(2,1)S(1)} all-to-all(bf16[16,8,2048]{2,1,0:T(8,128)(2,1)} %get-tuple-element.22), channel_id=1, replica_groups={{30,0,2,4,6,8,10,12,14,16,18,20,22,24,26,28},{31,1,3,5,7,9,11,13,15,17,..., dimensions={0} | all-to-all | bytes 1048576 | tf_op jit(solution)/shard_map/all_to_all | solution.py:300
  16.8 19.3 %all-to-all-start = ((bf16[16,16,512]{2,1,0:T(8,128)(2,1)}), bf16[16,16,512]{2,1,0:T(8,128)(2,1)S(1)}, u32[]{:S(2)}, u32[]{:S(2)}) async-start(bf16[16,16,512]{2,1,0:T(8,128)(2,1)} %get-tuple-element.20), calls=%async_computation | async-start | bytes 524288 | tf_op jit(solution)/shard_map/all_to_all | solution.py:300
  36.1 4.1 %collective-permute-start = (bf16[16,8,2048]{2,1,0:T(8,128)(2,1)S(1)}, bf16[16,8,2048]{2,1,0:T(8,128)(2,1)S(1)}, u32[]{:S(2)}, u32[]{:S(2)}) collective-permute-start(bf16[16,8,2048]{2,1,0:T(8,128)(2,1)S(1)} %all_to_all.30.mine_ref), channel_id=1, source_target_pairs={{0,1},{1,0},{2,3},{3,2},{4,5},{5,4},{6,7},{7,6},{8,9},{9,8},{10,11... | collective-permute-start | bytes 1572872 | tf_op jit(solution)/shard_map/ppermute | solution.py:309
  40.1 9.0 %all-to-all-done = bf16[16,16,512]{2,1,0:T(8,128)(2,1)S(1)} async-done(((bf16[16,16,512]{2,1,0:T(8,128)(2,1)}), bf16[16,16,512]{2,1,0:T(8,128)(2,1)S(1)}, u32[]{:S(2)}, u32[]{:S(2)}) %all-to-all-start) | async-done | bytes 262176 | tf_op jit(solution)/shard_map/all_to_all | solution.py:300
  49.1 0.0 collective-permute-done.other_ref
  49.1 0.0 copy-start.2
  49.1 0.7 copy-done.2
  49.8 4.7 %residual.1 = (bf16[2048,512]{1,0:T(8,128)(2,1)S(1)}, bf16[16,16,512]{2,1,0:T(8,128)(2,1)}, f32[8,512]{1,0:T(8,128)S(1)}) custom-call(s32[1]{0:T(128)} %bitcast.layer_ref, s32[4,16]{1,0:T(4,128)S(1)} %copy-done.2, bf16[16,8,2048]{2,1,0:T(8,128)(2,1)S(1)} %all_to_all.30.mine_ref, bf16[16,8,2048]{2,1,0:T(8,128)(2,1)S(1)} %collective-permute-done.other_ref, ...), custom_call_target="tpu_custom_call" | custom-call | flops 1073741824 | bytes 4194304 | tf_op jit(solution)/shard_map/residual/pallas_call | solution.py:123
  54.5 10.6 %all-to-all-start.3 = ((bf16[16,16,512]{2,1,0:T(8,128)(2,1)}), bf16[16,16,512]{2,1,0:T(8,128)(2,1)S(1)}, u32[]{:S(2)}, u32[]{:S(2)}) async-start(bf16[16,16,512]{2,1,0:T(8,128)(2,1)} %get-tuple-element.26), calls=%async_computation.3 | async-start | bytes 524288 | tf_op jit(solution)/shard_map/all_to_all | solution.py:300
  65.1 0.0 copy-start
  65.1 0.0 copy-start.1
  65.1 0.0 copy-start.3
  65.1 0.7 user_share.1
  65.9 3.7 %collective-permute-start.1 = (bf16[16,8,2048]{2,1,0:T(8,128)(2,1)S(1)}, bf16[16,8,2048]{2,1,0:T(8,128)(2,1)S(1)}, u32[]{:S(2)}, u32[]{:S(2)}) collective-permute-start(bf16[16,8,2048]{2,1,0:T(8,128)(2,1)S(1)} %get-tuple-element.25), channel_id=1, source_target_pairs={{0,1},{1,0},{2,3},{3,2},{4,5},{5,4},{6,7},{7,6},{8,9},{9,8},{10,11... | collective-permute-start | bytes 1572872 | tf_op jit(solution)/shard_map/ppermute | solution.py:309
  69.6 1.5 %collective-permute-done.1.arrived_ref = bf16[16,8,2048]{2,1,0:T(8,128)(2,1)S(1)} collective-permute-done((bf16[16,8,2048]{2,1,0:T(8,128)(2,1)S(1)}, bf16[16,8,2048]{2,1,0:T(8,128)(2,1)S(1)}, u32[]{:S(2)}, u32[]{:S(2)}) %collective-permute-start.1) | collective-permute-done | bytes 524320 | tf_op jit(solution)/shard_map/ppermute | solution.py:309
  71.1 0.9 halves.1
  72.0 6.8 %all-to-all-done.3.arrived_ref = bf16[16,16,512]{2,1,0:T(8,128)(2,1)S(1)} async-done(((bf16[16,16,512]{2,1,0:T(8,128)(2,1)}), bf16[16,16,512]{2,1,0:T(8,128)(2,1)S(1)}, u32[]{:S(2)}, u32[]{:S(2)}) %all-to-all-start.3) | async-done | bytes 262176 | tf_op jit(solution)/shard_map/all_to_all | solution.py:300
  78.8 7.9 %all-to-all-start.2 = ((bf16[16,8,2048]{2,1,0:T(8,128)(2,1)}), bf16[16,8,2048]{2,1,0:T(8,128)(2,1)S(1)}, u32[]{:S(2)}, u32[]{:S(2)}) async-start(bf16[16,8,2048]{2,1,0:T(8,128)(2,1)} %halves.1), calls=%async_computation.2 | async-start | bytes 1048576 | tf_op jit(solution)/shard_map/all_to_all | solution.py:300
  86.8 0.0 copy-done
  86.8 0.0 copy-done.1
  86.8 0.0 copy-done.3
  86.8 0.2 item_raw.1
  87.0 7.2 %all-to-all-done.2.arrived_ref = bf16[16,8,2048]{2,1,0:T(8,128)(2,1)S(1)} async-done(((bf16[16,8,2048]{2,1,0:T(8,128)(2,1)}), bf16[16,8,2048]{2,1,0:T(8,128)(2,1)S(1)}, u32[]{:S(2)}, u32[]{:S(2)}) %all-to-all-start.2) | async-done | bytes 524320 | tf_op jit(solution)/shard_map/all_to_all | solution.py:300
  94.2 0.2 user_raw.1
  94.4 12.2 %all_to_all.31.arrived_ref = f32[32,1,128]{2,1,0:T(1,128)S(1)} all-to-all(f32[32,1,128]{2,1,0:T(1,128)S(1)} %get-tuple-element.29), channel_id=1, replica_groups={{30,31,0,1,2,3,4,5,6,7,8,9,10,11,12,13,14,15,16,17,18,19,20,21,22,23,24..., dimensions={0} | all-to-all | bytes 32768 | tf_op jit(solution)/shard_map/all_to_all | solution.py:300
  106.6 12.8 %all_to_all.32.arrived_ref = f32[16,1,128]{2,1,0:T(1,128)S(1)} all-to-all(f32[16,1,128]{2,1,0:T(1,128)S(1)} %packed_again.1), channel_id=1, replica_groups={{256,288,320,352,384,416,448,480,0,32,64,96,128,160,192,224},{257,289,3..., dimensions={0} | all-to-all | bytes 16384 | tf_op jit(solution)/shard_map/all_to_all | solution.py:300
  119.5 0.8 step.1
  (1 shorter events, 0.0 us)
Async XLA Ops:
  16.8 32.3 %all-to-all-start = ((bf16[16,16,512]{2,1,0:T(8,128)(2,1)}), bf16[16,16,512]{2,1,0:T(8,128)(2,1)S(1)}, u32[]{:S(2)}, u32[]{:S(2)}) async-start(bf16[16,16,512]{2,1,0:T(8,128)(2,1)} %get-tuple-element.20), calls=%async_computation | async-start | bytes 524288 | tf_op jit(solution)/shard_map/all_to_all | solution.py:300
  36.1 13.1 %collective-permute-start = (bf16[16,8,2048]{2,1,0:T(8,128)(2,1)S(1)}, bf16[16,8,2048]{2,1,0:T(8,128)(2,1)S(1)}, u32[]{:S(2)}, u32[]{:S(2)}) collective-permute-start(bf16[16,8,2048]{2,1,0:T(8,128)(2,1)S(1)} %all_to_all.30.mine_ref), channel_id=1, source_target_pairs={{0,1},{1,0},{2,3},{3,2},{4,5},{5,4},{6,7},{7,6},{8,9},{9,8},{10,11... | collective-permute-start | bytes 1572872 | tf_op jit(solution)/shard_map/ppermute | solution.py:309
  49.1 0.7 copy-start.2
  54.5 24.3 %all-to-all-start.3 = ((bf16[16,16,512]{2,1,0:T(8,128)(2,1)}), bf16[16,16,512]{2,1,0:T(8,128)(2,1)S(1)}, u32[]{:S(2)}, u32[]{:S(2)}) async-start(bf16[16,16,512]{2,1,0:T(8,128)(2,1)} %get-tuple-element.26), calls=%async_computation.3 | async-start | bytes 524288 | tf_op jit(solution)/shard_map/all_to_all | solution.py:300
  65.1 21.7 %copy-start = (f32[8,2048]{1,0:T(8,128)S(1)}, f32[8,2048]{1,0:T(8,128)}, u32[]{:S(2)}) copy-start(f32[8,2048]{1,0:T(8,128)} %user_ref.5) | copy-start | bytes 196612
  65.1 21.7 %copy-start.1 = (f32[16,512]{1,0:T(8,128)S(1)}, f32[16,512]{1,0:T(8,128)}, u32[]{:S(2)}) copy-start(f32[16,512]{1,0:T(8,128)} %item_ref.5) | copy-start | bytes 98308
  65.1 21.7 %copy-start.3 = (s32[4,16]{1,0:T(4,128)S(1)}, s32[4,16]{1,0:T(4,128)}, u32[]{:S(2)}) copy-start(s32[4,16]{1,0:T(4,128)} %get-tuple-element.21.far_limits_ref.limits_ref) | copy-start | bytes 772
  65.9 5.2 %collective-permute-start.1 = (bf16[16,8,2048]{2,1,0:T(8,128)(2,1)S(1)}, bf16[16,8,2048]{2,1,0:T(8,128)(2,1)S(1)}, u32[]{:S(2)}, u32[]{:S(2)}) collective-permute-start(bf16[16,8,2048]{2,1,0:T(8,128)(2,1)S(1)} %get-tuple-element.25), channel_id=1, source_target_pairs={{0,1},{1,0},{2,3},{3,2},{4,5},{5,4},{6,7},{7,6},{8,9},{9,8},{10,11... | collective-permute-start | bytes 1572872 | tf_op jit(solution)/shard_map/ppermute | solution.py:309
  78.8 15.4 %all-to-all-start.2 = ((bf16[16,8,2048]{2,1,0:T(8,128)(2,1)}), bf16[16,8,2048]{2,1,0:T(8,128)(2,1)S(1)}, u32[]{:S(2)}, u32[]{:S(2)}) async-start(bf16[16,8,2048]{2,1,0:T(8,128)(2,1)} %halves.1), calls=%async_computation.2 | async-start | bytes 1048576 | tf_op jit(solution)/shard_map/all_to_all | solution.py:300
